TPU v7x, 128 devices: a whole 4x4x4 slice. The times are simulated.
128 devices in a mesh: shard: 128 (over z, y, x, core).
Axes of the slice: x: 4, y: 4, z: 4, core: 2. Of those that a mesh axis runs over, the one named last changes fastest.
Arguments:
- picked_rows: int32 [4096, 8], P('shard'), may hold values from 0 to 65535
- main_table: float32 [65536, 128], P('shard'), may hold values from -6 to 6
- dense_part: float32 [4096, 128], P('shard'), may hold values from -6 to 6
- small_ids: int32 [4096], P('shard'), may hold values from 0 to 511
- small_table: float32 [512, 128], P('shard'), may hold values from -6 to 6
- scale_ids: int32 [4096], P('shard'), may hold values from 0 to 511
Outputs:
- features: float32 [4096, 3, 128], P('shard')
All inputs are finite; a program needn't handle non-finite values.
Results may differ from a plain program's by a relative error of at most 0.0003.
Values sent between devices are 32-bit elements.
A program may use at most 64 MiB of HBM per device.

v0:
```python
import jax
import jax.numpy as jnp
from jax import lax
from jax.sharding import Mesh
from jax.sharding import PartitionSpec as P

PICKS = 8
SHARD = ("shard_0", "shard_1", "shard_2", "shard_3")


def joined_along(pieces, dim):
    shape = list(pieces.shape[1:])
    shape[dim] *= pieces.shape[0]
    return jnp.moveaxis(pieces, 0, dim).reshape(shape)


def all_blocks(x, axes, order):
    pieces = x
    for k in order:
        pieces = lax.all_gather(pieces, axes[k])
    done = order[::-1]
    back = [done.index(k) for k in range(len(axes))]
    pieces = pieces.transpose(*back, *range(len(axes), pieces.ndim))
    return pieces.reshape(-1, *x.shape)


def gather_axes(x, axes, order, dim):
    return joined_along(all_blocks(x, axes, order), dim)


def in_blocks(x, dim, length):
    shape = x.shape
    pieces = x.reshape(*shape[:dim], length, shape[dim] // length, *shape[dim + 1 :])
    return jnp.moveaxis(pieces, dim, 0)


def scatter_pairs(x, chips, core, dim):
    sizes = lax.axis_size(chips), lax.axis_size(core)
    pieces = in_blocks(x, dim, sizes[0] * sizes[1])
    inside = pieces.shape[1:]
    pieces = pieces.reshape(*sizes, *inside).swapaxes(0, 1).reshape(-1, *inside)
    pieces = lax.psum_scatter(pieces, core, scatter_dimension=0, tiled=True)
    return lax.psum_scatter(pieces, chips, scatter_dimension=0, tiled=True)[0]


def sum_by_chip(term, span, chips, core):
    total = term(jnp.int32(0), span * lax.axis_size(chips) * lax.axis_size(core))
    return scatter_pairs(total, chips, core, 0)


def rows_here(table_part, wanted, first_row):
    place = wanted - first_row
    inside = (place >= 0) & (place < table_part.shape[0])
    found = jnp.take(table_part, jnp.clip(place, 0, table_part.shape[0] - 1), axis=0).astype(
        jnp.float32
    )
    return jnp.where(inside[..., None], found, 0.0)


def on_device(picked_rows, main_table, dense_part, small_ids, small_table, scale_ids):
    big_first = lax.axis_index(SHARD) * main_table.shape[0]
    all_ids = gather_axes(picked_rows, SHARD, (0, 1, 2, 3), 0)

    def pooled_part(start, count):
        wanted = lax.dynamic_slice_in_dim(all_ids, start, count)
        return jnp.sum(rows_here(main_table, wanted, big_first), axis=1)

    pooled = sum_by_chip(
        pooled_part, picked_rows.shape[0], ("shard_0", "shard_1", "shard_2"), "shard_3"
    ) * PICKS ** (-0.5)
    every_row = gather_axes(small_table, SHARD, (0, 1, 2, 3), 0)
    small_rows = jnp.take(every_row, small_ids, axis=0).astype(jnp.float32)
    scale_rows = jnp.take(every_row, scale_ids, axis=0).astype(jnp.float32)
    dense_part = dense_part * scale_rows
    features = jnp.stack(
        [dense_part * pooled, pooled * small_rows, dense_part * small_rows], axis=1
    )
    return features


def solution(mesh):
    split = Mesh(mesh.devices.reshape(4, 4, 4, 2), ("shard_0", "shard_1", "shard_2", "shard_3"))
    placed = (P(SHARD, None), P(SHARD, None), P(SHARD, None), P(SHARD), P(SHARD, None), P(SHARD))
    return jax.shard_map(
        on_device, mesh=split, in_specs=placed, out_specs=P(SHARD, None, None), check_vma=False
    )
```

profile of v0, /device:TPU:0, one launch (start us, length us, event | category | flops | bytes accessed | tf_op | source)
XLA Modules:
  0.0 567.1 jit_solution(1485634945444086234)
XLA Ops:
  6.5 0.0 copy-start
  6.5 0.0 reduce-scatter.3.cloned.1.call-start
  6.5 13.4 %all-gather.9 = s32[4,32,8]{1,2,0:T(8,128)S(1)} all-gather(s32[1,32,8]{1,2,0:T(8,128)} %bitcast.60), channel_id=6, replica_groups=mesh['shard_0'=4,'shard_1'=4,'shard_2'=4,'shard_3'=2] {'shard_0'}, dimensions={0}, use_global_device_ids=true | all-gather | bytes 5120 | tf_op jit(solution)/shard_map/all_gather | solution.py:20
  20.0 12.4 %all-gather.5 = s32[16,32,8]{1,2,0:T(8,128)S(1)} all-gather(s32[4,32,8]{1,2,0:T(8,128)S(1)} %all-gather.9), channel_id=7, replica_groups=mesh['shard_0'=4,'shard_1'=4,'shard_2'=4,'shard_3'=2] {'shard_1'}, dimensions={0}, use_global_device_ids=true | all-gather | bytes 20480 | tf_op jit(solution)/shard_map/all_gather | solution.py:20
  32.3 12.6 %all-gather.6 = s32[16,4,32,8]{2,3,1,0:T(8,128)S(1)} all-gather(s32[4,4,32,8]{2,3,1,0:T(8,128)S(1)} %bitcast.58), channel_id=8, replica_groups=mesh['shard_0'=4,'shard_1'=4,'shard_2'=4,'shard_3'=2] {'shard_2'}, dimensions={0}, use_global_device_ids=true | all-gather | bytes 81920 | tf_op jit(solution)/shard_map/all_gather | solution.py:20
  44.9 2.2 all-gather.7
  47.1 0.1 subtract_clamp_fusion
  47.2 0.4 copy.31
  47.6 0.7 min.21
  48.3 0.7 min.19
  48.9 0.1 compare_and_fusion
  49.1 0.6 copy.34
  49.7 1.0 reshape.78
  50.8 0.8 copy.32
  51.6 0.3 copy.38
  51.9 1.0 copy.36
  52.9 0.0 copy-done
  52.9 109.0 %gather_fusion = f32[32768,128]{1,0:T(8,128)} fusion(f32[512,128]{1,0:T(8,128)S(1)} %copy-done, s32[32768]{0:T(1024)S(1)} %broadcast_clamp_fusion), kind=kCustom, calls=%fused_computation.2 | custom fusion | bytes 33685504 | tf_op jit(solution)/shard_map/jit(_take)/gather | solution.py:54
  161.9 0.0 copy-start.2
  161.9 0.0 copy-start.3
  161.9 0.0 copy-start.4
  161.9 0.0 copy-start.1
  161.9 24.1 %fusion.1 = f32[4096,128]{1,0:T(8,128)S(1)} fusion(f32[32768,128]{1,0:T(8,128)} %gather_fusion, pred[4096,8]{1,0:T(8,128)(4,1)S(1)} %copy.32, pred[4096,8]{1,0:T(8,128)(4,1)S(1)} %bitcast.49), kind=kLoop, calls=%fused_computation.5 | loop fusion | flops 12058624 | bytes 18939904 | tf_op jit(solution)/shard_map/reduce_sum | solution.py:66
  186.1 1.5 copy.35
  187.6 0.0 reduce-scatter.3.cloned.1.call-update
  187.6 0.0 reduce-scatter.5.cloned.1.call-start
  187.6 12.5 %reduce-scatter.3.cloned.1.call-done = f32[64,32,128]{2,1,0:T(8,128)} async-done(((f32[128,32,128]{2,1,0:T(8,128)}), f32[64,32,128]{2,1,0:T(8,128)}) %reduce-scatter.3.cloned.1.call-update) | async-done | bytes 1048592 | tf_op jit(solution)/shard_map/reduce_scatter | solution.py:42
  200.1 0.0 reduce-scatter.5.cloned.1.call-update
  200.2 0.0 copy-done.2
  200.2 12.4 %all-gather.8 = f32[4,4,128]{2,1,0:T(4,128)S(1)} all-gather(f32[1,4,128]{2,1,0:T(4,128)S(1)} %bitcast.61), channel_id=2, replica_groups=mesh['shard_0'=4,'shard_1'=4,'shard_2'=4,'shard_3'=2] {'shard_0'}, dimensions={0}, use_global_device_ids=true | all-gather | bytes 10240 | tf_op jit(solution)/shard_map/all_gather | solution.py:20
  212.6 12.2 %all-gather.1 = f32[16,4,128]{2,1,0:T(4,128)S(1)} all-gather(f32[4,4,128]{2,1,0:T(4,128)S(1)} %all-gather.8), channel_id=3, replica_groups=mesh['shard_0'=4,'shard_1'=4,'shard_2'=4,'shard_3'=2] {'shard_1'}, dimensions={0}, use_global_device_ids=true | all-gather | bytes 40960 | tf_op jit(solution)/shard_map/all_gather | solution.py:20
  224.7 12.3 %all-gather.2 = f32[16,4,4,128]{3,1,0,2:T(4,128)S(1)} all-gather(f32[4,4,4,128]{3,1,0,2:T(4,128)S(1)} %bitcast.59), channel_id=4, replica_groups=mesh['shard_0'=4,'shard_1'=4,'shard_2'=4,'shard_3'=2] {'shard_2'}, dimensions={0}, use_global_device_ids=true | all-gather | bytes 163840 | tf_op jit(solution)/shard_map/all_gather | solution.py:20
  237.1 2.0 all-gather.3
  239.1 0.1 copy.28
  239.2 0.0 copy-done.3
  239.2 0.6 gather_fusion.1
  239.8 0.0 copy-done.4
  239.8 0.6 gather_fusion.2
  240.4 318.5 %reduce-scatter.5.cloned.1.call-done = f32[1,32,128]{2,1,0:T(8,128)} async-done(((f32[64,32,128]{2,1,0:T(8,128)}), f32[1,32,128]{2,1,0:T(8,128)}) %reduce-scatter.5.cloned.1.call-update) | async-done | bytes 16400 | tf_op jit(solution)/shard_map/reduce_scatter | solution.py:43
  558.8 0.0 copy-done.1
  558.9 0.8 fusion.2
  559.6 0.6 pad_maximum_fusion
  (11 shorter events, 0.1 us)
Async XLA Ops:
  6.5 46.4 %copy-start = (f32[512,128]{1,0:T(8,128)S(1)}, f32[512,128]{1,0:T(8,128)}, u32[]{:S(2)}) copy-start(f32[512,128]{1,0:T(8,128)} %param.9) | copy-start | bytes 786436
  6.5 193.6 %reduce-scatter.3.cloned.1.call-start = ((), (), s32[]{:S(2)}) async-start(), calls=%async_computation.2 | async-start | bytes 3145728 | tf_op jit(solution)/shard_map/reduce_scatter | solution.py:42
  161.9 38.3 %copy-start.2 = (f32[4,128]{1,0:T(4,128)S(1)}, f32[4,128]{1,0:T(4,128)}, u32[]{:S(2)}) copy-start(f32[4,128]{1,0:T(4,128)} %param.12) | copy-start | bytes 6148
  161.9 77.2 %copy-start.3 = (s32[32]{0:T(128)S(1)}, s32[32]{0:T(128)}, u32[]{:S(2)}) copy-start(s32[32]{0:T(128)} %param.13) | copy-start | bytes 388
  161.9 77.8 %copy-start.4 = (s32[32]{0:T(128)S(1)}, s32[32]{0:T(128)}, u32[]{:S(2)}) copy-start(s32[32]{0:T(128)} %param.11) | copy-start | bytes 388
  161.9 396.9 %copy-start.1 = (f32[32,128]{1,0:T(8,128)S(1)}, f32[32,128]{1,0:T(8,128)}, u32[]{:S(2)}) copy-start(f32[32,128]{1,0:T(8,128)} %param.10) | copy-start | bytes 49156
  187.6 371.3 %reduce-scatter.5.cloned.1.call-start = ((), (), s32[]{:S(2)}) async-start(), calls=%async_computation.3 | async-start | bytes 1064960 | tf_op jit(solution)/shard_map/reduce_scatter | solution.py:43
Sparse Core Ops, SparseCore 0:
  187.7 12.3 reduce-scatter.2
  202.5 356.3 reduce-scatter.4
where the time goes:
time: 567 us
  waiting for transfers between devices  331 us (58%)
  local copies, waits for them, and re-layouts  117 us (21%)
  blocking collectives  79.4 us (14%)
  other arithmetic  25.9 us (5%)
  between operations  13.6 us (2%)
    reduce_scatter x1, waiting for transfers between devices, scatter_pairs(): return lax.psum_scatter(pieces, chips, scatter_dimension=0, tiled=True)[0]  318 us
    gather x1, local copies, waits for them, and re-layouts, rows_here(): jnp.take(table_part, jnp.clip(place, 0, table_part.shape[0] - 1), axis=0)  109 us
    all_gather x8, blocking collectives, all_blocks(): pieces = lax.all_gather(pieces, axes[k])  79.4 us
    reduce_sum x1, other arithmetic, pooled_part(): return jnp.sum(rows_here(main_table, wanted, big_first), axis=1)  24.1 us
    reduce_scatter x1, waiting for transfers between devices, scatter_pairs(): pieces = lax.psum_scatter(pieces, core, scatter_dimension=0, tiled=True)  12.5 us
  transfers between devices with their start and end apart: 2, of which 2 were waited for; matrix products, arithmetic and copies ran while one was open for 0% of the time, Pallas kernels for 0%

commit v1 on v0

v1 whole, which is shorter than its diff:
```python
import functools

import jax
import jax.numpy as jnp
from jax import lax
from jax.experimental import pallas as pl
from jax.experimental.pallas import tpu as pltpu
from jax.sharding import Mesh
from jax.sharding import PartitionSpec as P

PICKS = 8
SHARD = ("z", "y", "x", "c")
MESH = pl.DeviceIdType.MESH


def kernel(
    picks_hbm, table_hbm, dense_hbm, small_hbm, small_ids, scale_ids,
    out_ref,
    picks_in, ids, ids_t, count, table, split, total, part, got, small, dense, lhs_rows, scale_rows,
    load_sem, ids_send, ids_recv, tab_send, tab_recv, core_send, core_recv,
    small_send, small_recv, sum_send, sum_recv,
):
    z, y, x, c = (lax.axis_index(a) for a in SHARD)
    zy = z * 4 + y

    def peer(dz=0, dy=0, dx=0, dc=0):
        return (
            lax.rem(z + dz, 4), lax.rem(y + dy, 4), lax.rem(x + dx, 4), lax.rem(c + dc, 2)
        )

    def at_x(s):
        return lax.rem(x + 4 - s, 4)

    def send(src, dst, send_sem, recv_sem, to):
        copy = pltpu.make_async_remote_copy(
            src_ref=src, dst_ref=dst, send_sem=send_sem, recv_sem=recv_sem,
            device_id=to, device_id_type=MESH,
        )
        copy.start()
        return copy

    half = 256
    load_picks = pltpu.make_async_copy(picks_hbm, picks_in, load_sem.at[0])
    load_table = pltpu.make_async_copy(table_hbm, table.at[x, c], load_sem.at[1])
    load_small = pltpu.make_async_copy(small_hbm, small.at[c, x, zy], load_sem.at[2])
    load_dense = pltpu.make_async_copy(dense_hbm, dense, load_sem.at[3])
    load_table.start()
    load_picks.start()
    load_small.start()
    load_dense.start()

    axis_peers = (
        [peer(dx=d) for d in (1, 2, 3)] + [peer(dc=1)]
        + [peer(dy=d) for d in (1, 2, 3)] + [peer(dz=d) for d in (1, 2, 3)]
    )
    barrier = pltpu.get_barrier_semaphore()
    for who in axis_peers:
        pl.semaphore_signal(barrier, inc=1, device_id=who, device_id_type=MESH)
    pl.semaphore_wait(barrier, len(axis_peers))

    started = []

    def table_piece(s, h, core):
        return table.at[at_x(s), core, pl.ds(h * half, half)]

    def ring(s, h, step):
        piece = table_piece(s, h, c)
        k = ((s * 2 + h) * 2) + (0 if step == 1 else 1)
        copy = send(piece, piece, tab_send.at[k], tab_recv.at[k], peer(dx=step % 4))
        started.append(copy)
        return copy

    def arrived(k, piece, sem):
        pltpu.make_async_copy(piece, piece, sem.at[k]).wait()

    def cross(k, piece):
        started.append(send(piece, piece, core_send.at[k], core_recv.at[k], peer(dc=1)))

    load_table.wait()
    ring(0, 0, 1)
    ring(0, 1, -1)
    ring(0, 1, 1)
    ring(0, 0, -1)
    cross(0, table.at[x, c])

    load_picks.wait()
    ids[zy] = picks_in[...]
    load_small.wait()
    for d in (1, 2, 3):
        started.append(send(ids.at[zy], ids.at[zy], ids_send.at[d], ids_recv.at[d], peer(dy=d)))
        started.append(send(
            small.at[c, x, zy], small.at[c, x, zy], small_send.at[d], small_recv.at[d], peer(dy=d)
        ))
    for d in (1, 2, 3):
        came = z * 4 + lax.rem(y + 4 - d, 4)
        arrived(d, ids.at[came], ids_recv)
        arrived(d, small.at[c, x, came], small_recv)
    mine = pl.ds(z * 4, 4)
    for d in (1, 2, 3):
        started.append(send(
            ids.at[mine], ids.at[mine], ids_send.at[3 + d], ids_recv.at[3 + d], peer(dz=d)
        ))
        started.append(send(
            small.at[c, x, mine], small.at[c, x, mine],
            small_send.at[3 + d], small_recv.at[3 + d], peer(dz=d),
        ))

    def recv_index(s, h, step):
        return ((s * 2 + h) * 2) + (0 if step == 1 else 1)

    arrived(recv_index(0, 0, 1), table_piece(1, 0, c), tab_recv)
    ring(1, 0, 1)
    arrived(recv_index(0, 1, -1), table_piece(3, 1, c), tab_recv)
    ring(3, 1, -1)
    cross(1, table_piece(1, 0, c))
    cross(2, table_piece(3, 1, c))

    for d in (1, 2, 3):
        came = pl.ds(lax.rem(z + 4 - d, 4) * 4, 4)
        arrived(3 + d, ids.at[came], ids_recv)
        arrived(3 + d, small.at[c, x, came], small_recv)
    for d in (1, 2, 3):
        started.append(send(
            small.at[c, x], small.at[c, x], small_send.at[6 + d], small_recv.at[6 + d], peer(dx=d)
        ))

    first = zy * 4096
    for b in range(16):
        block = ids[b] - first
        block = jnp.concatenate([block, jnp.zeros((8, 96), jnp.int32)], axis=1)
        ids_t[b * 32 : (b + 1) * 32, :] = jnp.concatenate(
            [jnp.transpose(block)[:32], jnp.zeros((32, 120), jnp.int32)], axis=1
        )

    lane = lax.broadcasted_iota(jnp.int32, (8, 128), 1)

    def count_rows(s):
        base = at_x(s) * 1024

        def tile(t, carry):
            halves = []
            for u in range(2):
                rows = ids_t[pl.ds(pl.multiple_of(t * 16 + u * 8, 8), 8), :] - base
                halves.append([
                    jnp.broadcast_to(rows[:, k : k + 1], (8, 128)) for k in range(PICKS)
                ])
            for q in range(8):
                sums = []
                for u in range(2):
                    acc = None
                    for k in range(PICKS):
                        hit = jnp.where(halves[u][k] == lane + q * 128, 1.0, 0.0)
                        acc = hit if acc is None else acc + hit
                    sums.append(acc)
                count[s, pl.ds(pl.multiple_of(t * 16, 16), 16), q * 128 : (q + 1) * 128] = (
                    jnp.concatenate(sums, axis=0).astype(jnp.bfloat16)
                )
            return carry

        lax.fori_loop(0, 32, tile, 0)

    def add_product(s, start):
        for core in range(2):
            def cut(t, carry):
                at = pl.ds(pl.multiple_of(t * 64, 64), 64)
                rows = table[at_x(s), core, at]
                high = rows.astype(jnp.bfloat16)
                low = (rows - high.astype(jnp.float32)).astype(jnp.bfloat16)
                split[core, at, 0:128] = high
                split[core, at, 128:256] = low
                return carry

            lax.fori_loop(0, 8, cut, 0)

        def tile(t, carry):
            at = pl.ds(pl.multiple_of(t * 128, 128), 128)
            new = jnp.dot(
                count[s, at, :], split[...].reshape(1024, 256), preferred_element_type=jnp.float32
            )
            if start:
                total[at, :] = new
            else:
                total[at, :] = total[at, :] + new
            return carry

        lax.fori_loop(0, 4, tile, 0)

    count_rows(0)
    arrived(recv_index(0, 1, 1), table_piece(1, 1, c), tab_recv)
    cross(3, table_piece(1, 1, c))
    arrived(recv_index(0, 0, -1), table_piece(3, 0, c), tab_recv)
    cross(4, table_piece(3, 0, c))
    for d in (1, 2, 3):
        arrived(6 + d, small.at[c, at_x(d)], small_recv)
    started.append(send(small.at[c], small.at[c], small_send.at[10], small_recv.at[10], peer(dc=1)))
    count_rows(1)
    count_rows(2)
    arrived(recv_index(1, 0, 1), table_piece(2, 0, c), tab_recv)
    cross(5, table_piece(2, 0, c))
    arrived(recv_index(3, 1, -1), table_piece(2, 1, c), tab_recv)
    cross(6, table_piece(2, 1, c))
    count_rows(3)

    o = 1 - c
    arrived(0, table.at[x, o], core_recv)
    add_product(0, True)
    arrived(1, table_piece(1, 0, o), core_recv)
    arrived(3, table_piece(1, 1, o), core_recv)
    add_product(1, False)
    arrived(2, table_piece(3, 1, o), core_recv)
    arrived(4, table_piece(3, 0, o), core_recv)
    add_product(3, False)
    arrived(5, table_piece(2, 0, o), core_recv)
    arrived(6, table_piece(2, 1, o), core_recv)
    add_product(2, False)
    part[...] = (total[:, :128] + total[:, 128:]).reshape(16, 32, 128)

    for j in range(1, 16):
        dz, dy = divmod(j, 4)
        to = peer(dz=dz, dy=dy)
        started.append(send(
            part.at[to[0] * 4 + to[1]], got.at[j], sum_send.at[j], sum_recv.at[j], to
        ))

    arrived(10, small.at[o], small_recv)
    load_dense.wait()

    def small_row(i):
        core, place = lax.rem(lax.div(i, 4), 2), lax.rem(lax.div(i, 8), 4)
        return small[core, place, lax.div(i, 32), pl.ds(lax.rem(i, 4), 1), :]

    for e in range(32):
        lhs_rows[e : e + 1, :] = small_row(small_ids[e])
        scale_rows[e : e + 1, :] = small_row(scale_ids[e])
    rows = lhs_rows[...]
    scaled = dense[...] * scale_rows[...]
    out_ref[2] = scaled * rows

    pooled = part[zy]
    for j in range(1, 16):
        arrived(j, got.at[j], sum_recv)
        pooled = pooled + got[j]
    pooled = pooled * PICKS ** (-0.5)
    out_ref[0] = scaled * pooled
    out_ref[1] = pooled * rows
    for copy in started:
        copy.wait_send()


def on_device(picked_rows, main_table, dense_part, small_ids, small_table, scale_ids):
    dma = pltpu.SemaphoreType.DMA
    f32 = jnp.float32
    out = pl.pallas_call(
        kernel,
        out_shape=jax.ShapeDtypeStruct((3, 32, 128), f32),
        in_specs=[pl.BlockSpec(memory_space=pl.ANY)] * 4
        + [pl.BlockSpec(memory_space=pltpu.SMEM)] * 2,
        out_specs=pl.BlockSpec(memory_space=pltpu.VMEM),
        scratch_shapes=[
            pltpu.VMEM((8, 32), jnp.int32),
            pltpu.VMEM((16, 8, 32), jnp.int32),
            pltpu.VMEM((512, 128), jnp.int32),
            pltpu.VMEM((4, 512, 1024), jnp.bfloat16),
            pltpu.VMEM((4, 2, 512, 128), f32),
            pltpu.VMEM((2, 512, 256), jnp.bfloat16),
            pltpu.VMEM((512, 256), f32),
            pltpu.VMEM((16, 32, 128), f32),
            pltpu.VMEM((16, 32, 128), f32),
            pltpu.VMEM((2, 4, 16, 4, 128), f32),
            pltpu.VMEM((32, 128), f32),
            pltpu.VMEM((32, 128), f32),
            pltpu.VMEM((32, 128), f32),
            dma((4,)), dma((7,)), dma((7,)), dma((16,)), dma((16,)), dma((7,)), dma((7,)),
            dma((11,)), dma((11,)), dma((16,)), dma((16,)),
        ],
        compiler_params=pltpu.CompilerParams(collective_id=0, has_side_effects=True),
    )(picked_rows.T, main_table, dense_part, small_table, small_ids, scale_ids)
    return out.transpose(1, 0, 2)


def solution(mesh):
    split = Mesh(mesh.devices.reshape(4, 4, 4, 2), SHARD)
    placed = (P(SHARD, None), P(SHARD, None), P(SHARD, None), P(SHARD), P(SHARD, None), P(SHARD))
    return jax.shard_map(
        on_device, mesh=split, in_specs=placed, out_specs=P(SHARD, None, None), check_vma=False
    )
```

time: 567 us -> 44.7 us (0.08)
  waiting for transfers between devices: 331 us -> 0 us
  local copies, waits for them, and re-layouts: 117 us -> 1.42 us
  blocking collectives: 79.4 us -> 0 us
  Pallas kernels: 0 us -> 43.1 us
  other arithmetic: 25.9 us -> 0 us
  between operations: 13.6 us -> 0.01 us
    reduce_scatter x2 -> x0, waiting for transfers between devices: 331 us -> none  [the longest x1 318 us: scatter_pairs(): return lax.psum_scatter(pieces, chips, scatter_dimension=0, tiled=True)[0]]
    gather x3 -> x0, local copies, waits for them, and re-layouts: 110 us -> none  [the longest x1 109 us: rows_here(): jnp.take(table_part, jnp.clip(place, 0, table_part.shape[0] - 1), axis=0)]
    all_gather x8 -> x0, blocking collectives: 79.4 us -> none  [all_blocks(): pieces = lax.all_gather(pieces, axes[k])]
    pallas_call x0 -> x1, Pallas kernels: none -> 43.1 us  [on_device(): pl.pallas_call(kernel, out_shape=jax.ShapeDtypeStruct((3, 32, 128), f32),...]
    reduce_sum x1 -> x0, other arithmetic: 24.1 us -> none  [pooled_part(): return jnp.sum(rows_here(main_table, wanted, big_first), axis=1)]
  transfers between devices with their start and end apart: 2 -> 0, of which waited for: 2 -> 0; matrix products, arithmetic and copies ran while one was open for 0% -> 0% of each run, Pallas kernels for 0% -> 0%
where the time goes in v1:
time: 44.7 us; the launch traced here: 44.5 us
  Pallas kernels  43.1 us (96%)
  local copies, waits for them, and re-layouts  1.42 us (3%)
    pallas_call x1, Pallas kernels, on_device(): pl.pallas_call(kernel, out_shape=jax.ShapeDtypeStruct((3, 32, 128), f32),...  43.1 us
    unnamed x1, local copies, waits for them, and re-layouts  1.42 us

profile of v1, /device:TPU:0, one launch (start us, length us, event | category | flops | bytes accessed | tf_op | source)
XLA Modules:
  0.0 44.5 jit_solution(15632844593179652220)
XLA Ops:
  0.0 43.1 %shard_map.64 = f32[3,32,128]{2,1,0:T(8,128)} custom-call(s32[8,32]{1,0:T(8,128)} %bitcast.3, f32[512,128]{1,0:T(8,128)} %table_hbm.1, f32[32,128]{1,0:T(8,128)} %dense_hbm.1, f32[4,128]{1,0:T(4,128)} %small_hbm.1, s32[32]{0:T(128)} %small_ids.1, s32[32]{0:T(128)} %scale_ids.1), custom_call_target="tpu_custom_call" | custom-call | tf_op jit(solution)/shard_map/pallas_call | solution.py:253
  43.1 1.4 %copy.8 = f32[32,3,128]{2,0,1:T(8,128)} copy(f32[32,3,128]{2,0,1:T(8,128)} %bitcast.2) | data formatting | bytes 98304

commit v2 on v1

--- a/solution.py
+++ b/solution.py
@@ -14,9 +14,9 @@
 
 
 def kernel(
-    picks_hbm, table_hbm, dense_hbm, small_hbm, small_ids, scale_ids,
+    picks_hbm, table_hbm, dense_hbm, small_hbm, small_ids_hbm, scale_ids_hbm,
     out_ref,
-    picks_in, ids, ids_t, count, table, split, total, part, got, small, dense, lhs_rows, scale_rows,
+    small_ids, scale_ids, picks_in, ids, spread, count, table, split, total, part, got, small, dense, lhs_rows, scale_rows,
     load_sem, ids_send, ids_recv, tab_send, tab_recv, core_send, core_recv,
     small_send, small_recv, sum_send, sum_recv,
 ):
@@ -48,6 +48,12 @@
     load_picks.start()
     load_small.start()
     load_dense.start()
+    load_ids = [
+        pltpu.make_async_copy(small_ids_hbm, small_ids, load_sem.at[4]),
+        pltpu.make_async_copy(scale_ids_hbm, scale_ids, load_sem.at[5]),
+    ]
+    for load in load_ids:
+        load.start()
 
     axis_peers = (
         [peer(dx=d) for d in (1, 2, 3)] + [peer(dc=1)]
@@ -126,66 +132,50 @@
 
     first = zy * 4096
     for b in range(16):
-        block = ids[b] - first
+        block = jnp.clip(ids[b] - first, -1, 4096)
         block = jnp.concatenate([block, jnp.zeros((8, 96), jnp.int32)], axis=1)
-        ids_t[b * 32 : (b + 1) * 32, :] = jnp.concatenate(
-            [jnp.transpose(block)[:32], jnp.zeros((32, 120), jnp.int32)], axis=1
+        columns = jnp.transpose(block)[:32]
+        for k in range(PICKS):
+            spread[k, b * 32 : (b + 1) * 32, :] = jnp.broadcast_to(
+                columns[:, k : k + 1], (32, 128)
+            ).astype(jnp.int16)
+    one, none = jnp.ones((16, 128), jnp.bfloat16), jnp.zeros((16, 128), jnp.bfloat16)
+    lane = lax.broadcasted_iota(jnp.int32, (16, 128), 1).astype(jnp.int16)
+
+    def count_rows(places):
+        def tile(t, carry):
+            at = pl.ds(pl.multiple_of(t * 16, 16), 16)
+            wanted = [spread[k, at, :] for k in range(PICKS)]
+            for place in places:
+                for q in range(8):
+                    here = lane + jnp.int16(place * 1024 + q * 128)
+                    hits = [jnp.where(w == here, one, none) for w in wanted]
+                    while len(hits) > 1:
+                        hits = [a + b for a, b in zip(hits[::2], hits[1::2])]
+                    count[place, at, q * 128 : (q + 1) * 128] = hits[0]
+            return carry
+
+        lax.fori_loop(0, 32, tile, 0)
+
+    def cut_rows(s, core):
+        def cut(t, carry):
+            at = pl.ds(pl.multiple_of(t * 128, 128), 128)
+            rows = table[at_x(s), core, at]
+            high = rows.astype(jnp.bfloat16)
+            low = (rows - high.astype(jnp.float32)).astype(jnp.bfloat16)
+            split[s, core, at, 0:128] = high
+            split[s, core, at, 128:256] = low
+            return carry
+
+        lax.fori_loop(0, 4, cut, 0)
+
+    def add_product(s, start):
+        new = jnp.dot(
+            count[at_x(s)], split[s].reshape(1024, 256), preferred_element_type=jnp.float32
         )
-
-    lane = lax.broadcasted_iota(jnp.int32, (8, 128), 1)
-
-    def count_rows(s):
-        base = at_x(s) * 1024
-
-        def tile(t, carry):
-            halves = []
-            for u in range(2):
-                rows = ids_t[pl.ds(pl.multiple_of(t * 16 + u * 8, 8), 8), :] - base
-                halves.append([
-                    jnp.broadcast_to(rows[:, k : k + 1], (8, 128)) for k in range(PICKS)
-                ])
-            for q in range(8):
-                sums = []
-                for u in range(2):
-                    acc = None
-                    for k in range(PICKS):
-                        hit = jnp.where(halves[u][k] == lane + q * 128, 1.0, 0.0)
-                        acc = hit if acc is None else acc + hit
-                    sums.append(acc)
-                count[s, pl.ds(pl.multiple_of(t * 16, 16), 16), q * 128 : (q + 1) * 128] = (
-                    jnp.concatenate(sums, axis=0).astype(jnp.bfloat16)
-                )
-            return carry
-
-        lax.fori_loop(0, 32, tile, 0)
-
-    def add_product(s, start):
-        for core in range(2):
-            def cut(t, carry):
-                at = pl.ds(pl.multiple_of(t * 64, 64), 64)
-                rows = table[at_x(s), core, at]
-                high = rows.astype(jnp.bfloat16)
-                low = (rows - high.astype(jnp.float32)).astype(jnp.bfloat16)
-                split[core, at, 0:128] = high
-                split[core, at, 128:256] = low
-                return carry
-
-            lax.fori_loop(0, 8, cut, 0)
-
-        def tile(t, carry):
-            at = pl.ds(pl.multiple_of(t * 128, 128), 128)
-            new = jnp.dot(
-                count[s, at, :], split[...].reshape(1024, 256), preferred_element_type=jnp.float32
-            )
-            if start:
-                total[at, :] = new
-            else:
-                total[at, :] = total[at, :] + new
-            return carry
-
-        lax.fori_loop(0, 4, tile, 0)
-
-    count_rows(0)
+        total[...] = new if start else total[...] + new
+
+    count_rows((0, 1))
     arrived(recv_index(0, 1, 1), table_piece(1, 1, c), tab_recv)
     cross(3, table_piece(1, 1, c))
     arrived(recv_index(0, 0, -1), table_piece(3, 0, c), tab_recv)
@@ -193,25 +183,30 @@
     for d in (1, 2, 3):
         arrived(6 + d, small.at[c, at_x(d)], small_recv)
     started.append(send(small.at[c], small.at[c], small_send.at[10], small_recv.at[10], peer(dc=1)))
-    count_rows(1)
-    count_rows(2)
+    count_rows((2, 3))
+    o = 1 - c
+    cut_rows(0, c)
+    arrived(0, table.at[x, o], core_recv)
+    cut_rows(0, o)
+    add_product(0, True)
     arrived(recv_index(1, 0, 1), table_piece(2, 0, c), tab_recv)
     cross(5, table_piece(2, 0, c))
     arrived(recv_index(3, 1, -1), table_piece(2, 1, c), tab_recv)
     cross(6, table_piece(2, 1, c))
-    count_rows(3)
-
-    o = 1 - c
-    arrived(0, table.at[x, o], core_recv)
-    add_product(0, True)
     arrived(1, table_piece(1, 0, o), core_recv)
     arrived(3, table_piece(1, 1, o), core_recv)
+    cut_rows(1, c)
+    cut_rows(1, o)
     add_product(1, False)
     arrived(2, table_piece(3, 1, o), core_recv)
     arrived(4, table_piece(3, 0, o), core_recv)
+    cut_rows(3, c)
+    cut_rows(3, o)
     add_product(3, False)
+    cut_rows(2, c)
     arrived(5, table_piece(2, 0, o), core_recv)
     arrived(6, table_piece(2, 1, o), core_recv)
+    cut_rows(2, o)
     add_product(2, False)
     part[...] = (total[:, :128] + total[:, 128:]).reshape(16, 32, 128)
 
@@ -224,6 +219,8 @@
 
     arrived(10, small.at[o], small_recv)
     load_dense.wait()
+    for load in load_ids:
+        load.wait()
 
     def small_row(i):
         core, place = lax.rem(lax.div(i, 4), 2), lax.rem(lax.div(i, 8), 4)
@@ -252,17 +249,18 @@
     f32 = jnp.float32
     out = pl.pallas_call(
         kernel,
-        out_shape=jax.ShapeDtypeStruct((3, 32, 128), f32),
-        in_specs=[pl.BlockSpec(memory_space=pl.ANY)] * 4
-        + [pl.BlockSpec(memory_space=pltpu.SMEM)] * 2,
+        out_shape=pltpu.VMEM((3, 32, 128), f32),
+        in_specs=[pl.BlockSpec(memory_space=pl.ANY)] * 6,
         out_specs=pl.BlockSpec(memory_space=pltpu.VMEM),
         scratch_shapes=[
+            pltpu.SMEM((32,), jnp.int32),
+            pltpu.SMEM((32,), jnp.int32),
             pltpu.VMEM((8, 32), jnp.int32),
             pltpu.VMEM((16, 8, 32), jnp.int32),
-            pltpu.VMEM((512, 128), jnp.int32),
+            pltpu.VMEM((8, 512, 128), jnp.int16),
             pltpu.VMEM((4, 512, 1024), jnp.bfloat16),
             pltpu.VMEM((4, 2, 512, 128), f32),
-            pltpu.VMEM((2, 512, 256), jnp.bfloat16),
+            pltpu.VMEM((4, 2, 512, 256), jnp.bfloat16),
             pltpu.VMEM((512, 256), f32),
             pltpu.VMEM((16, 32, 128), f32),
             pltpu.VMEM((16, 32, 128), f32),
@@ -270,7 +268,7 @@
             pltpu.VMEM((32, 128), f32),
             pltpu.VMEM((32, 128), f32),
             pltpu.VMEM((32, 128), f32),
-            dma((4,)), dma((7,)), dma((7,)), dma((16,)), dma((16,)), dma((7,)), dma((7,)),
+            dma((6,)), dma((7,)), dma((7,)), dma((16,)), dma((16,)), dma((7,)), dma((7,)),
             dma((11,)), dma((11,)), dma((16,)), dma((16,)),
         ],
         compiler_params=pltpu.CompilerParams(collective_id=0, has_side_effects=True),

time: 44.7 us -> 33.1 us (0.74)
  Pallas kernels: 43.1 us -> 32.4 us
  local copies, waits for them, and re-layouts: 1.42 us -> 0.62 us
    pallas_call x1, Pallas kernels: 43.1 us -> 32.4 us  [on_device(): pl.pallas_call(kernel, out_shape=pltpu.VMEM((3, 32, 128), f32), in_specs=...]
    unnamed x1, local copies, waits for them, and re-layouts: 1.42 us -> 0.62 us
where the time goes in v2:
time: 33.1 us; the launch traced here: 33 us
  Pallas kernels  32.4 us (98%)
  local copies, waits for them, and re-layouts  0.62 us (2%)
    pallas_call x1, Pallas kernels, on_device(): pl.pallas_call(kernel, out_shape=pltpu.VMEM((3, 32, 128), f32), in_specs=...  32.4 us

profile of v2, /device:TPU:0, one launch (start us, length us, event | category | flops | bytes accessed | tf_op | source)
XLA Modules:
  0.0 33.0 jit_solution(15752316341026974721)
XLA Ops:
  0.0 32.4 %shard_map.64 = f32[3,32,128]{2,1,0:T(8,128)S(1)} custom-call(s32[8,32]{1,0:T(8,128)} %bitcast.3, f32[512,128]{1,0:T(8,128)} %table_hbm.1, f32[32,128]{1,0:T(8,128)} %dense_hbm.1, f32[4,128]{1,0:T(4,128)} %small_hbm.1, s32[32]{0:T(128)} %small_ids_hbm.1, s32[32]{0:T(128)} %scale_ids_hbm.1), custom_call_target="tpu_custom_call" | custom-call | tf_op jit(solution)/shard_map/pallas_call | solution.py:250
  32.4 0.6 %copy.8 = f32[32,3,128]{2,0,1:T(8,128)} copy(f32[32,3,128]{2,0,1:T(8,128)S(1)} %bitcast.2) | data formatting | bytes 98304

commit v3 on v2

--- a/solution.py
+++ b/solution.py
@@ -111,51 +111,35 @@
             small_send.at[3 + d], small_recv.at[3 + d], peer(dz=d),
         ))
 
-    def recv_index(s, h, step):
-        return ((s * 2 + h) * 2) + (0 if step == 1 else 1)
-
-    arrived(recv_index(0, 0, 1), table_piece(1, 0, c), tab_recv)
-    ring(1, 0, 1)
-    arrived(recv_index(0, 1, -1), table_piece(3, 1, c), tab_recv)
-    ring(3, 1, -1)
-    cross(1, table_piece(1, 0, c))
-    cross(2, table_piece(3, 1, c))
-
-    for d in (1, 2, 3):
-        came = pl.ds(lax.rem(z + 4 - d, 4) * 4, 4)
-        arrived(3 + d, ids.at[came], ids_recv)
-        arrived(3 + d, small.at[c, x, came], small_recv)
-    for d in (1, 2, 3):
-        started.append(send(
-            small.at[c, x], small.at[c, x], small_send.at[6 + d], small_recv.at[6 + d], peer(dx=d)
-        ))
-
     first = zy * 4096
-    for b in range(16):
-        block = jnp.clip(ids[b] - first, -1, 4096)
-        block = jnp.concatenate([block, jnp.zeros((8, 96), jnp.int32)], axis=1)
-        columns = jnp.transpose(block)[:32]
-        for k in range(PICKS):
-            spread[k, b * 32 : (b + 1) * 32, :] = jnp.broadcast_to(
-                columns[:, k : k + 1], (32, 128)
-            ).astype(jnp.int16)
-    one, none = jnp.ones((16, 128), jnp.bfloat16), jnp.zeros((16, 128), jnp.bfloat16)
-    lane = lax.broadcasted_iota(jnp.int32, (16, 128), 1).astype(jnp.int16)
-
-    def count_rows(places):
+
+    def spread_picks(plane):
+        for b in range(4):
+            block = jnp.clip(ids[plane * 4 + b] - first, -1, 4096)
+            block = jnp.concatenate([block, jnp.zeros((8, 96), jnp.int32)], axis=1)
+            columns = jnp.transpose(block)[:32]
+            for k in range(PICKS):
+                spread[k, plane, b * 32 : (b + 1) * 32, :] = jnp.broadcast_to(
+                    columns[:, k : k + 1], (32, 256)
+                ).astype(jnp.int16)
+
+    one, none = jnp.ones((16, 256), jnp.bfloat16), jnp.zeros((16, 256), jnp.bfloat16)
+    lane = lax.broadcasted_iota(jnp.int32, (16, 256), 1).astype(jnp.int16)
+
+    def count_rows(plane):
         def tile(t, carry):
             at = pl.ds(pl.multiple_of(t * 16, 16), 16)
-            wanted = [spread[k, at, :] for k in range(PICKS)]
-            for place in places:
-                for q in range(8):
-                    here = lane + jnp.int16(place * 1024 + q * 128)
+            wanted = [spread[k, plane, at, :] for k in range(PICKS)]
+            for place in range(4):
+                for q in range(4):
+                    here = lane + jnp.int16(place * 1024 + q * 256)
                     hits = [jnp.where(w == here, one, none) for w in wanted]
                     while len(hits) > 1:
                         hits = [a + b for a, b in zip(hits[::2], hits[1::2])]
-                    count[place, at, q * 128 : (q + 1) * 128] = hits[0]
+                    count[place, plane, at, q * 256 : (q + 1) * 256] = hits[0]
             return carry
 
-        lax.fori_loop(0, 32, tile, 0)
+        lax.fori_loop(0, 8, tile, 0)
 
     def cut_rows(s, core):
         def cut(t, carry):
@@ -171,21 +155,39 @@
 
     def add_product(s, start):
         new = jnp.dot(
-            count[at_x(s)], split[s].reshape(1024, 256), preferred_element_type=jnp.float32
+            count[at_x(s)].reshape(512, 1024), split[s].reshape(1024, 256), preferred_element_type=jnp.float32
         )
         total[...] = new if start else total[...] + new
 
-    count_rows((0, 1))
+    def recv_index(s, h, step):
+        return ((s * 2 + h) * 2) + (0 if step == 1 else 1)
+
+    spread_picks(z)
+    count_rows(z)
+    o = 1 - c
+    cut_rows(0, c)
+    arrived(recv_index(0, 0, 1), table_piece(1, 0, c), tab_recv)
+    ring(1, 0, 1)
+    arrived(recv_index(0, 1, -1), table_piece(3, 1, c), tab_recv)
+    ring(3, 1, -1)
+    cross(1, table_piece(1, 0, c))
+    cross(2, table_piece(3, 1, c))
+
+    for d in (1, 2, 3):
+        came = lax.rem(z + 4 - d, 4)
+        arrived(3 + d, ids.at[pl.ds(came * 4, 4)], ids_recv)
+        spread_picks(came)
+        count_rows(came)
     arrived(recv_index(0, 1, 1), table_piece(1, 1, c), tab_recv)
     cross(3, table_piece(1, 1, c))
     arrived(recv_index(0, 0, -1), table_piece(3, 0, c), tab_recv)
     cross(4, table_piece(3, 0, c))
     for d in (1, 2, 3):
-        arrived(6 + d, small.at[c, at_x(d)], small_recv)
-    started.append(send(small.at[c], small.at[c], small_send.at[10], small_recv.at[10], peer(dc=1)))
-    count_rows((2, 3))
-    o = 1 - c
-    cut_rows(0, c)
+        arrived(3 + d, small.at[c, x, pl.ds(lax.rem(z + 4 - d, 4) * 4, 4)], small_recv)
+    for d in (1, 2, 3):
+        started.append(send(
+            small.at[c, x], small.at[c, x], small_send.at[6 + d], small_recv.at[6 + d], peer(dx=d)
+        ))
     arrived(0, table.at[x, o], core_recv)
     cut_rows(0, o)
     add_product(0, True)
@@ -217,6 +219,9 @@
             part.at[to[0] * 4 + to[1]], got.at[j], sum_send.at[j], sum_recv.at[j], to
         ))
 
+    for d in (1, 2, 3):
+        arrived(6 + d, small.at[c, at_x(d)], small_recv)
+    started.append(send(small.at[c], small.at[c], small_send.at[10], small_recv.at[10], peer(dc=1)))
     arrived(10, small.at[o], small_recv)
     load_dense.wait()
     for load in load_ids:
@@ -257,8 +262,8 @@
             pltpu.SMEM((32,), jnp.int32),
             pltpu.VMEM((8, 32), jnp.int32),
             pltpu.VMEM((16, 8, 32), jnp.int32),
-            pltpu.VMEM((8, 512, 128), jnp.int16),
-            pltpu.VMEM((4, 512, 1024), jnp.bfloat16),
+            pltpu.VMEM((8, 4, 128, 256), jnp.int16),
+            pltpu.VMEM((4, 4, 128, 1024), jnp.bfloat16),
             pltpu.VMEM((4, 2, 512, 128), f32),
             pltpu.VMEM((4, 2, 512, 256), jnp.bfloat16),
             pltpu.VMEM((512, 256), f32),

time: 33.1 us -> 28.5 us (0.86)
  Pallas kernels: 32.4 us -> 27.8 us
    pallas_call x1, Pallas kernels: 32.4 us -> 27.8 us  [on_device(): pl.pallas_call(kernel, out_shape=pltpu.VMEM((3, 32, 128), f32), in_specs=...]
where the time goes in v3:
time: 28.5 us; the launch traced here: 28.4 us
  Pallas kernels  27.8 us (98%)
  local copies, waits for them, and re-layouts  0.62 us (2%)
    pallas_call x1, Pallas kernels, on_device(): pl.pallas_call(kernel, out_shape=pltpu.VMEM((3, 32, 128), f32), in_specs=...  27.8 us
    unnamed x1, local copies, waits for them, and re-layouts  0.62 us

profile of v3, /device:TPU:0, one launch (start us, length us, event | category | flops | bytes accessed | tf_op | source)
XLA Modules:
  0.0 28.4 jit_solution(10933271922686757958)
XLA Ops:
  0.0 27.8 %shard_map.64 = f32[3,32,128]{2,1,0:T(8,128)S(1)} custom-call(s32[8,32]{1,0:T(8,128)} %bitcast.3, f32[512,128]{1,0:T(8,128)} %table_hbm.1, f32[32,128]{1,0:T(8,128)} %dense_hbm.1, f32[4,128]{1,0:T(4,128)} %small_hbm.1, s32[32]{0:T(128)} %small_ids_hbm.1, s32[32]{0:T(128)} %scale_ids_hbm.1), custom_call_target="tpu_custom_call" | custom-call | tf_op jit(solution)/shard_map/pallas_call | solution.py:255
  27.8 0.6 %copy.8 = f32[32,3,128]{2,0,1:T(8,128)} copy(f32[32,3,128]{2,0,1:T(8,128)S(1)} %bitcast.2) | data formatting | bytes 98304

commit v4 on v3

--- a/solution.py
+++ b/solution.py
@@ -64,52 +64,42 @@
         pl.semaphore_signal(barrier, inc=1, device_id=who, device_id_type=MESH)
     pl.semaphore_wait(barrier, len(axis_peers))
 
-    started = []
 
     def table_piece(s, h, core):
         return table.at[at_x(s), core, pl.ds(h * half, half)]
 
-    def ring(s, h, step):
+    def ring(s, h, step, k):
         piece = table_piece(s, h, c)
-        k = ((s * 2 + h) * 2) + (0 if step == 1 else 1)
-        copy = send(piece, piece, tab_send.at[k], tab_recv.at[k], peer(dx=step % 4))
-        started.append(copy)
-        return copy
+        send(piece, piece, tab_send.at[0], tab_recv.at[k], peer(dx=step % 4))
 
     def arrived(k, piece, sem):
         pltpu.make_async_copy(piece, piece, sem.at[k]).wait()
 
     def cross(k, piece):
-        started.append(send(piece, piece, core_send.at[k], core_recv.at[k], peer(dc=1)))
-
-    load_table.wait()
-    ring(0, 0, 1)
-    ring(0, 1, -1)
-    ring(0, 1, 1)
-    ring(0, 0, -1)
-    cross(0, table.at[x, c])
+        send(piece, piece, core_send.at[0], core_recv.at[k], peer(dc=1))
 
     load_picks.wait()
     ids[zy] = picks_in[...]
+    for d in (2, 1, 3):
+        send(ids.at[zy], ids.at[zy], ids_send.at[0], ids_recv.at[0], peer(dy=d))
+    load_table.wait()
+    ring(0, 0, 1, 0)
+    ring(0, 1, -1, 1)
+    ring(0, 1, 1, 2)
+    ring(0, 0, -1, 3)
+    cross(0, table.at[x, c])
     load_small.wait()
+    for d in (2, 1, 3):
+        own = small.at[c, x, zy]
+        send(own, own, small_send.at[0], small_recv.at[0], peer(dy=d))
+    arrived(0, ids.at[pl.ds(0, 3)], ids_recv)
+    mine = pl.ds(z * 4, 4)
+    for d in (2, 1, 3):
+        send(ids.at[mine], ids.at[mine], ids_send.at[1], ids_recv.at[d], peer(dz=d))
+    arrived(0, small.at[0, 0, pl.ds(0, 3)], small_recv)
     for d in (1, 2, 3):
-        started.append(send(ids.at[zy], ids.at[zy], ids_send.at[d], ids_recv.at[d], peer(dy=d)))
-        started.append(send(
-            small.at[c, x, zy], small.at[c, x, zy], small_send.at[d], small_recv.at[d], peer(dy=d)
-        ))
-    for d in (1, 2, 3):
-        came = z * 4 + lax.rem(y + 4 - d, 4)
-        arrived(d, ids.at[came], ids_recv)
-        arrived(d, small.at[c, x, came], small_recv)
-    mine = pl.ds(z * 4, 4)
-    for d in (1, 2, 3):
-        started.append(send(
-            ids.at[mine], ids.at[mine], ids_send.at[3 + d], ids_recv.at[3 + d], peer(dz=d)
-        ))
-        started.append(send(
-            small.at[c, x, mine], small.at[c, x, mine],
-            small_send.at[3 + d], small_recv.at[3 + d], peer(dz=d),
-        ))
+        own = small.at[c, x, mine]
+        send(own, own, small_send.at[1], small_recv.at[1], peer(dz=d))
 
     first = zy * 4096
 
@@ -147,82 +137,82 @@
             rows = table[at_x(s), core, at]
             high = rows.astype(jnp.bfloat16)
             low = (rows - high.astype(jnp.float32)).astype(jnp.bfloat16)
-            split[s, core, at, 0:128] = high
-            split[s, core, at, 128:256] = low
+            split[(0, 1, 3, 2)[s], core, at, 0:128] = high
+            split[(0, 1, 3, 2)[s], core, at, 128:256] = low
             return carry
 
         lax.fori_loop(0, 4, cut, 0)
-
-    def add_product(s, start):
-        new = jnp.dot(
-            count[at_x(s)].reshape(512, 1024), split[s].reshape(1024, 256), preferred_element_type=jnp.float32
-        )
-        total[...] = new if start else total[...] + new
-
-    def recv_index(s, h, step):
-        return ((s * 2 + h) * 2) + (0 if step == 1 else 1)
 
     spread_picks(z)
     count_rows(z)
     o = 1 - c
     cut_rows(0, c)
-    arrived(recv_index(0, 0, 1), table_piece(1, 0, c), tab_recv)
-    ring(1, 0, 1)
-    arrived(recv_index(0, 1, -1), table_piece(3, 1, c), tab_recv)
-    ring(3, 1, -1)
+    arrived(0, table_piece(1, 0, c), tab_recv)
+    ring(1, 0, 1, 4)
     cross(1, table_piece(1, 0, c))
+    arrived(1, table_piece(3, 1, c), tab_recv)
+    ring(3, 1, -1, 5)
     cross(2, table_piece(3, 1, c))
-
-    for d in (1, 2, 3):
+    def take_plane(d):
         came = lax.rem(z + 4 - d, 4)
-        arrived(3 + d, ids.at[pl.ds(came * 4, 4)], ids_recv)
         spread_picks(came)
         count_rows(came)
-    arrived(recv_index(0, 1, 1), table_piece(1, 1, c), tab_recv)
-    cross(3, table_piece(1, 1, c))
-    arrived(recv_index(0, 0, -1), table_piece(3, 0, c), tab_recv)
-    cross(4, table_piece(3, 0, c))
-    for d in (1, 2, 3):
-        arrived(3 + d, small.at[c, x, pl.ds(lax.rem(z + 4 - d, 4) * 4, 4)], small_recv)
-    for d in (1, 2, 3):
-        started.append(send(
-            small.at[c, x], small.at[c, x], small_send.at[6 + d], small_recv.at[6 + d], peer(dx=d)
-        ))
+
+    def ids_from(d):
+        return ids.at[pl.ds(lax.rem(z + 4 - d, 4) * 4, 4)]
+
+    arrived(1, ids_from(1), ids_recv)
+    take_plane(1)
+    arrived(3, ids_from(3), ids_recv)
+    take_plane(3)
+    arrived(2, table_piece(1, 1, c), tab_recv)
+    cross(1, table_piece(1, 1, c))
+    arrived(3, table_piece(3, 0, c), tab_recv)
+    cross(2, table_piece(3, 0, c))
+    arrived(2, ids_from(2), ids_recv)
+    take_plane(2)
+    arrived(1, small.at[0, 0, pl.ds(0, 12)], small_recv)
+    for d in (2, 1, 3):
+        own = small.at[c, x]
+        send(own, own, small_send.at[2], small_recv.at[2], peer(dx=d))
     arrived(0, table.at[x, o], core_recv)
     cut_rows(0, o)
-    add_product(0, True)
-    arrived(recv_index(1, 0, 1), table_piece(2, 0, c), tab_recv)
-    cross(5, table_piece(2, 0, c))
-    arrived(recv_index(3, 1, -1), table_piece(2, 1, c), tab_recv)
-    cross(6, table_piece(2, 1, c))
-    arrived(1, table_piece(1, 0, o), core_recv)
-    arrived(3, table_piece(1, 1, o), core_recv)
     cut_rows(1, c)
+    cut_rows(3, c)
+    arrived(1, table.at[at_x(1), o], core_recv)
+    arrived(2, table.at[at_x(3), o], core_recv)
     cut_rows(1, o)
-    add_product(1, False)
-    arrived(2, table_piece(3, 1, o), core_recv)
-    arrived(4, table_piece(3, 0, o), core_recv)
-    cut_rows(3, c)
     cut_rows(3, o)
-    add_product(3, False)
+    arrived(4, table_piece(2, 0, c), tab_recv)
+    cross(3, table_piece(2, 0, c))
+    arrived(5, table_piece(2, 1, c), tab_recv)
+    cross(3, table_piece(2, 1, c))
+    total[...] = jnp.dot(
+        jnp.concatenate([count[at_x(s)].reshape(512, 1024) for s in (0, 1, 3)], axis=1),
+        split[0:3].reshape(3072, 256),
+        preferred_element_type=jnp.float32,
+    ).reshape(4, 128, 256)
     cut_rows(2, c)
-    arrived(5, table_piece(2, 0, o), core_recv)
-    arrived(6, table_piece(2, 1, o), core_recv)
+    arrived(3, table.at[at_x(2), o], core_recv)
     cut_rows(2, o)
-    add_product(2, False)
-    part[...] = (total[:, :128] + total[:, 128:]).reshape(16, 32, 128)
-
-    for j in range(1, 16):
-        dz, dy = divmod(j, 4)
-        to = peer(dz=dz, dy=dy)
-        started.append(send(
-            part.at[to[0] * 4 + to[1]], got.at[j], sum_send.at[j], sum_recv.at[j], to
-        ))
-
-    for d in (1, 2, 3):
-        arrived(6 + d, small.at[c, at_x(d)], small_recv)
-    started.append(send(small.at[c], small.at[c], small_send.at[10], small_recv.at[10], peer(dc=1)))
-    arrived(10, small.at[o], small_recv)
+    last = split[3].reshape(1024, 256)
+    for dz in (2, 1, 3, 0):
+        plane = lax.rem(z + dz, 4)
+        new = total[plane] + jnp.dot(
+            count[at_x(2), plane], last, preferred_element_type=jnp.float32
+        )
+        part[pl.ds(plane * 4, 4)] = (new[:, :128] + new[:, 128:]).reshape(4, 32, 128)
+        for dy in (2, 1, 3, 0):
+            if dz or dy:
+                to = peer(dz=dz, dy=dy)
+                send(
+                    part.at[to[0] * 4 + to[1]], got.at[dz * 4 + dy],
+                    sum_send.at[0], sum_recv.at[0], to,
+                )
+    arrived(2, small.at[0, pl.ds(0, 3)], small_recv)
+    own = small.at[c]
+    send(own, own, small_send.at[3], small_recv.at[3], peer(dc=1))
+    arrived(3, small.at[o], small_recv)
     load_dense.wait()
     for load in load_ids:
         load.wait()
@@ -239,14 +229,21 @@
     out_ref[2] = scaled * rows
 
     pooled = part[zy]
+    arrived(0, got.at[pl.ds(1, 15)], sum_recv)
     for j in range(1, 16):
-        arrived(j, got.at[j], sum_recv)
         pooled = pooled + got[j]
     pooled = pooled * PICKS ** (-0.5)
     out_ref[0] = scaled * pooled
     out_ref[1] = pooled * rows
-    for copy in started:
-        copy.wait_send()
+    arrived(0, table.at[pl.ds(0, 3), 0], tab_send)
+    arrived(0, table.at[:, 0], core_send)
+    arrived(0, ids.at[pl.ds(0, 3)], ids_send)
+    arrived(1, ids.at[pl.ds(0, 12)], ids_send)
+    arrived(0, small.at[0, 0, pl.ds(0, 3)], small_send)
+    arrived(1, small.at[0, 0, pl.ds(0, 12)], small_send)
+    arrived(2, small.at[0, pl.ds(0, 3)], small_send)
+    arrived(3, small.at[0], small_send)
+    arrived(0, got.at[pl.ds(1, 15)], sum_send)
 
 
 def on_device(picked_rows, main_table, dense_part, small_ids, small_table, scale_ids):
@@ -266,15 +263,15 @@
             pltpu.VMEM((4, 4, 128, 1024), jnp.bfloat16),
             pltpu.VMEM((4, 2, 512, 128), f32),
             pltpu.VMEM((4, 2, 512, 256), jnp.bfloat16),
-            pltpu.VMEM((512, 256), f32),
+            pltpu.VMEM((4, 128, 256), f32),
             pltpu.VMEM((16, 32, 128), f32),
             pltpu.VMEM((16, 32, 128), f32),
             pltpu.VMEM((2, 4, 16, 4, 128), f32),
             pltpu.VMEM((32, 128), f32),
             pltpu.VMEM((32, 128), f32),
             pltpu.VMEM((32, 128), f32),
-            dma((6,)), dma((7,)), dma((7,)), dma((16,)), dma((16,)), dma((7,)), dma((7,)),
-            dma((11,)), dma((11,)), dma((16,)), dma((16,)),
+            dma((6,)), dma((2,)), dma((4,)), dma((1,)), dma((6,)), dma((1,)), dma((4,)),
+            dma((4,)), dma((4,)), dma((1,)), dma((1,)),
         ],
         compiler_params=pltpu.CompilerParams(collective_id=0, has_side_effects=True),
     )(picked_rows.T, main_table, dense_part, small_table, small_ids, scale_ids)

time: 28.5 us -> 26.4 us (0.926)
  Pallas kernels: 27.8 us -> 25.7 us
    pallas_call x1, Pallas kernels: 27.8 us -> 25.7 us  [on_device(): pl.pallas_call(kernel, out_shape=pltpu.VMEM((3, 32, 128), f32), in_specs=...]
where the time goes in v4:
time: 26.4 us; the launch traced here: 26.3 us
  Pallas kernels  25.7 us (97%)
  local copies, waits for them, and re-layouts  0.62 us (2%)
    pallas_call x1, Pallas kernels, on_device(): pl.pallas_call(kernel, out_shape=pltpu.VMEM((3, 32, 128), f32), in_specs=...  25.7 us
    unnamed x1, local copies, waits for them, and re-layouts  0.62 us

profile of v4, /device:TPU:0, one launch (start us, length us, event | category | flops | bytes accessed | tf_op | source)
XLA Modules:
  0.0 26.3 jit_solution(17368692205462848750)
XLA Ops:
  0.0 25.7 %shard_map.64 = f32[3,32,128]{2,1,0:T(8,128)S(1)} custom-call(s32[8,32]{1,0:T(8,128)} %bitcast.3, f32[512,128]{1,0:T(8,128)} %table_hbm.1, f32[32,128]{1,0:T(8,128)} %dense_hbm.1, f32[4,128]{1,0:T(4,128)} %small_hbm.1, s32[32]{0:T(128)} %small_ids_hbm.1, s32[32]{0:T(128)} %scale_ids_hbm.1), custom_call_target="tpu_custom_call" | custom-call | tf_op jit(solution)/shard_map/pallas_call | solution.py:252
  25.7 0.6 %copy.8 = f32[32,3,128]{2,0,1:T(8,128)} copy(f32[32,3,128]{2,0,1:T(8,128)S(1)} %bitcast.2) | data formatting | bytes 98304

commit v5 on v4

--- a/solution.py
+++ b/solution.py
@@ -126,7 +126,7 @@
                     hits = [jnp.where(w == here, one, none) for w in wanted]
                     while len(hits) > 1:
                         hits = [a + b for a, b in zip(hits[::2], hits[1::2])]
-                    count[place, plane, at, q * 256 : (q + 1) * 256] = hits[0]
+                    count[place, q // 2, plane, at, q % 2 * 256 : (q % 2 + 1) * 256] = hits[0]
             return carry
 
         lax.fori_loop(0, 8, tile, 0)
@@ -161,10 +161,10 @@
     def ids_from(d):
         return ids.at[pl.ds(lax.rem(z + 4 - d, 4) * 4, 4)]
 
+    arrived(3, ids_from(3), ids_recv)
+    take_plane(3)
     arrived(1, ids_from(1), ids_recv)
     take_plane(1)
-    arrived(3, ids_from(3), ids_recv)
-    take_plane(3)
     arrived(2, table_piece(1, 1, c), tab_recv)
     cross(1, table_piece(1, 1, c))
     arrived(3, table_piece(3, 0, c), tab_recv)
@@ -179,27 +179,32 @@
     cut_rows(0, o)
     cut_rows(1, c)
     cut_rows(3, c)
+    def product(pieces):
+        lhs = [count[at_x(s), core].reshape(512, 512) for s, core in pieces]
+        rhs = [split[(0, 1, 3, 2)[s], core] for s, core in pieces]
+        return jnp.dot(
+            jnp.concatenate(lhs, axis=1), jnp.concatenate(rhs, axis=0),
+            preferred_element_type=jnp.float32,
+        ).reshape(4, 128, 256)
+
+    arrived(4, table_piece(2, 0, c), tab_recv)
+    cross(3, table_piece(2, 0, c))
+    arrived(5, table_piece(2, 1, c), tab_recv)
+    cross(3, table_piece(2, 1, c))
+    total[...] = product(((0, c), (0, o), (1, c), (3, c)))
     arrived(1, table.at[at_x(1), o], core_recv)
     arrived(2, table.at[at_x(3), o], core_recv)
     cut_rows(1, o)
     cut_rows(3, o)
-    arrived(4, table_piece(2, 0, c), tab_recv)
-    cross(3, table_piece(2, 0, c))
-    arrived(5, table_piece(2, 1, c), tab_recv)
-    cross(3, table_piece(2, 1, c))
-    total[...] = jnp.dot(
-        jnp.concatenate([count[at_x(s)].reshape(512, 1024) for s in (0, 1, 3)], axis=1),
-        split[0:3].reshape(3072, 256),
-        preferred_element_type=jnp.float32,
-    ).reshape(4, 128, 256)
     cut_rows(2, c)
+    total[...] = total[...] + product(((1, o), (3, o), (2, c)))
     arrived(3, table.at[at_x(2), o], core_recv)
     cut_rows(2, o)
-    last = split[3].reshape(1024, 256)
+    last = split[3, o]
     for dz in (2, 1, 3, 0):
         plane = lax.rem(z + dz, 4)
         new = total[plane] + jnp.dot(
-            count[at_x(2), plane], last, preferred_element_type=jnp.float32
+            count[at_x(2), o, plane], last, preferred_element_type=jnp.float32
         )
         part[pl.ds(plane * 4, 4)] = (new[:, :128] + new[:, 128:]).reshape(4, 32, 128)
         for dy in (2, 1, 3, 0):
@@ -260,7 +265,7 @@
             pltpu.VMEM((8, 32), jnp.int32),
             pltpu.VMEM((16, 8, 32), jnp.int32),
             pltpu.VMEM((8, 4, 128, 256), jnp.int16),
-            pltpu.VMEM((4, 4, 128, 1024), jnp.bfloat16),
+            pltpu.VMEM((4, 2, 4, 128, 512), jnp.bfloat16),
             pltpu.VMEM((4, 2, 512, 128), f32),
             pltpu.VMEM((4, 2, 512, 256), jnp.bfloat16),
             pltpu.VMEM((4, 128, 256), f32),

time: 26.4 us -> 26.1 us (0.989)
  Pallas kernels: 25.7 us -> 25.3 us
    pallas_call x1, Pallas kernels: 25.7 us -> 25.3 us  [on_device(): pl.pallas_call(kernel, out_shape=pltpu.VMEM((3, 32, 128), f32), in_specs=...]
where the time goes in v5:
time: 26.1 us; the launch traced here: 26 us
  Pallas kernels  25.3 us (97%)
  local copies, waits for them, and re-layouts  0.62 us (2%)
    pallas_call x1, Pallas kernels, on_device(): pl.pallas_call(kernel, out_shape=pltpu.VMEM((3, 32, 128), f32), in_specs=...  25.3 us
    unnamed x1, local copies, waits for them, and re-layouts  0.62 us

profile of v5, /device:TPU:0, one launch (start us, length us, event | category | flops | bytes accessed | tf_op | source)
XLA Modules:
  0.0 26.0 jit_solution(7920582666717925732)
XLA Ops:
  0.0 25.3 %shard_map.64 = f32[3,32,128]{2,1,0:T(8,128)S(1)} custom-call(s32[8,32]{1,0:T(8,128)} %bitcast.3, f32[512,128]{1,0:T(8,128)} %table_hbm.1, f32[32,128]{1,0:T(8,128)} %dense_hbm.1, f32[4,128]{1,0:T(4,128)} %small_hbm.1, s32[32]{0:T(128)} %small_ids_hbm.1, s32[32]{0:T(128)} %scale_ids_hbm.1), custom_call_target="tpu_custom_call" | custom-call | tf_op jit(solution)/shard_map/pallas_call | solution.py:257
  25.3 0.6 %copy.8 = f32[32,3,128]{2,0,1:T(8,128)} copy(f32[32,3,128]{2,0,1:T(8,128)S(1)} %bitcast.2) | data formatting | bytes 98304

commit v6 on v5

--- a/solution.py
+++ b/solution.py
@@ -56,8 +56,8 @@
         load.start()
 
     axis_peers = (
-        [peer(dx=d) for d in (1, 2, 3)] + [peer(dc=1)]
-        + [peer(dy=d) for d in (1, 2, 3)] + [peer(dz=d) for d in (1, 2, 3)]
+        [peer(dz=d) for d in (2, 1, 3)] + [peer(dy=d) for d in (2, 1, 3)]
+        + [peer(dx=d) for d in (2, 1, 3)] + [peer(dc=1)]
     )
     barrier = pltpu.get_barrier_semaphore()
     for who in axis_peers:
@@ -201,19 +201,20 @@
     arrived(3, table.at[at_x(2), o], core_recv)
     cut_rows(2, o)
     last = split[3, o]
-    for dz in (2, 1, 3, 0):
-        plane = lax.rem(z + dz, 4)
-        new = total[plane] + jnp.dot(
-            count[at_x(2), o, plane], last, preferred_element_type=jnp.float32
-        )
-        part[pl.ds(plane * 4, 4)] = (new[:, :128] + new[:, 128:]).reshape(4, 32, 128)
-        for dy in (2, 1, 3, 0):
-            if dz or dy:
-                to = peer(dz=dz, dy=dy)
-                send(
-                    part.at[to[0] * 4 + to[1]], got.at[dz * 4 + dy],
-                    sum_send.at[0], sum_recv.at[0], to,
-                )
+    for pair in ((2, 1), (3, 0)):
+        planes = [lax.rem(z + dz, 4) for dz in pair]
+        lhs = jnp.concatenate([count[at_x(2), o, plane] for plane in planes], axis=0)
+        new = jnp.dot(lhs, last, preferred_element_type=jnp.float32)
+        for n, (dz, plane) in enumerate(zip(pair, planes)):
+            here = total[plane] + new[n * 128 : (n + 1) * 128]
+            part[pl.ds(plane * 4, 4)] = (here[:, :128] + here[:, 128:]).reshape(4, 32, 128)
+            for dy in (2, 1, 3, 0):
+                if dz or dy:
+                    to = peer(dz=dz, dy=dy)
+                    send(
+                        part.at[to[0] * 4 + to[1]], got.at[dz * 4 + dy],
+                        sum_send.at[0], sum_recv.at[0], to,
+                    )
     arrived(2, small.at[0, pl.ds(0, 3)], small_recv)
     own = small.at[c]
     send(own, own, small_send.at[3], small_recv.at[3], peer(dc=1))

time: 26.1 us -> 26.1 us (level)
  no operation moved by 1% of the time
where the time goes in v6:
time: 26.1 us; the launch traced here: 26 us
  Pallas kernels  25.3 us (97%)
  local copies, waits for them, and re-layouts  0.62 us (2%)
    pallas_call x1, Pallas kernels, on_device(): pl.pallas_call(kernel, out_shape=pltpu.VMEM((3, 32, 128), f32), in_specs=...  25.3 us
    unnamed x1, local copies, waits for them, and re-layouts  0.62 us

profile of v6, /device:TPU:0, one launch (start us, length us, event | category | flops | bytes accessed | tf_op | source)
XLA Modules:
  0.0 26.0 jit_solution(5087769486587537949)
XLA Ops:
  0.0 25.3 %shard_map.64 = f32[3,32,128]{2,1,0:T(8,128)S(1)} custom-call(s32[8,32]{1,0:T(8,128)} %bitcast.3, f32[512,128]{1,0:T(8,128)} %table_hbm.1, f32[32,128]{1,0:T(8,128)} %dense_hbm.1, f32[4,128]{1,0:T(4,128)} %small_hbm.1, s32[32]{0:T(128)} %small_ids_hbm.1, s32[32]{0:T(128)} %scale_ids_hbm.1), custom_call_target="tpu_custom_call" | custom-call | tf_op jit(solution)/shard_map/pallas_call | solution.py:258
  25.4 0.6 %copy.8 = f32[32,3,128]{2,0,1:T(8,128)} copy(f32[32,3,128]{2,0,1:T(8,128)S(1)} %bitcast.2) | data formatting | bytes 98304

commit v7 on v6

--- a/solution.py
+++ b/solution.py
@@ -177,6 +177,10 @@
         send(own, own, small_send.at[2], small_recv.at[2], peer(dx=d))
     arrived(0, table.at[x, o], core_recv)
     cut_rows(0, o)
+    arrived(4, table_piece(2, 0, c), tab_recv)
+    cross(3, table_piece(2, 0, c))
+    arrived(5, table_piece(2, 1, c), tab_recv)
+    cross(3, table_piece(2, 1, c))
     cut_rows(1, c)
     cut_rows(3, c)
     def product(pieces):
@@ -187,10 +191,6 @@
             preferred_element_type=jnp.float32,
         ).reshape(4, 128, 256)
 
-    arrived(4, table_piece(2, 0, c), tab_recv)
-    cross(3, table_piece(2, 0, c))
-    arrived(5, table_piece(2, 1, c), tab_recv)
-    cross(3, table_piece(2, 1, c))
     total[...] = product(((0, c), (0, o), (1, c), (3, c)))
     arrived(1, table.at[at_x(1), o], core_recv)
     arrived(2, table.at[at_x(3), o], core_recv)

time: 26.1 us -> 26.1 us (level)
  no operation moved by 1% of the time
where the time goes in v7:
time: 26.1 us; the launch traced here: 26 us
  Pallas kernels  25.4 us (97%)
  local copies, waits for them, and re-layouts  0.62 us (2%)
    pallas_call x1, Pallas kernels, on_device(): pl.pallas_call(kernel, out_shape=pltpu.VMEM((3, 32, 128), f32), in_specs=...  25.4 us
    unnamed x1, local copies, waits for them, and re-layouts  0.62 us

profile of v7, /device:TPU:0, one launch (start us, length us, event | category | flops | bytes accessed | tf_op | source)
XLA Modules:
  0.0 26.0 jit_solution(5789083080762456222)
XLA Ops:
  0.0 25.4 %shard_map.64 = f32[3,32,128]{2,1,0:T(8,128)S(1)} custom-call(s32[8,32]{1,0:T(8,128)} %bitcast.3, f32[512,128]{1,0:T(8,128)} %table_hbm.1, f32[32,128]{1,0:T(8,128)} %dense_hbm.1, f32[4,128]{1,0:T(4,128)} %small_hbm.1, s32[32]{0:T(128)} %small_ids_hbm.1, s32[32]{0:T(128)} %scale_ids_hbm.1), custom_call_target="tpu_custom_call" | custom-call | tf_op jit(solution)/shard_map/pallas_call | solution.py:258
  25.4 0.6 %copy.8 = f32[32,3,128]{2,0,1:T(8,128)} copy(f32[32,3,128]{2,0,1:T(8,128)S(1)} %bitcast.2) | data formatting | bytes 98304
